TPU v7x, 32 devices: a whole 2x2x4 slice. The times are simulated.
32 devices in a mesh: orient: 8 (over z, y), dom: 4 (over x, core).
Axes of the slice: x: 2, y: 2, z: 4, core: 2. Of those that a mesh axis runs over, the one named last changes fastest.
Arguments:
- particles: bfloat16 [256, 8448], P(('dom', 'orient')), parts along dimension 0, may hold values from -12 to 12
- defocus: float32 [256], P(('dom', 'orient')), parts along dimension 0, may hold values from 10 to 60
- inv_noise: float32 [4224], replicated, may hold values from 0.5 to 2
- references: bfloat16 [13824, 8448], P(('dom', 'orient')), parts along dimension 0, may hold values from -0.25 to 0.25
- thresholds: int32 [256], P('dom'), parts along dimension 0, may hold values from 512 to 1023
- range_start: int32 [256], P('dom'), parts along dimension 0, may hold values from 0 to 3455
- range_len: int32 [256], P('dom'), parts along dimension 0, may hold values from 36 to 1727
Outputs:
- posterior: float32 [256, 3456], P('dom', 'orient'), parts along dimension 0
- cumulative: float32 [256, 3456], P('dom', 'orient'), parts along dimension 0
- log_evidence: float32 [256], P('dom'), parts along dimension 0
- kept_mass: float32 [256], P('dom'), parts along dimension 0
There are 4 independent parts, one for each index of `dom`. A program takes and returns all parts, laid end to end along the dimension named above; an argument that names none is the same for every part. Nothing has to cross between parts.
All inputs are finite; a program needn't handle non-finite values.
Results may differ from a plain program's by a relative error of at most 0.0004.
The roundings to bfloat16 on the way count: a program that leaves them out, or rounds other values in their place, can miss the bound.
Values may be sent and summed in bfloat16 or wider, within the bound.
A program may use at most 64 MiB of HBM per device.

v0:
```python
import math

import jax
import jax.numpy as jnp
from jax import lax
from jax.sharding import PartitionSpec as P


def ctf_table(defocus, coef):
    index = jnp.arange(coef, dtype=jnp.int32)
    row_pos = (index // 128).astype(jnp.float32)
    col_pos = (index % 128 - 64).astype(jnp.float32)
    freq = math.pi * (row_pos * row_pos + col_pos * col_pos) / 16384.0
    return -jnp.sin(defocus[:, None] * freq[None, :] + 0.07)


def on_device(particles, defocus, inv_noise, references, thresholds, range_start, range_len):
    coef = inv_noise.shape[0]
    feat = 2 * coef
    ori_dev = references.shape[0]
    ctf = ctf_table(defocus, coef)
    ctf_both = jnp.concatenate([ctf, ctf], axis=1)
    noise_both = jnp.concatenate([inv_noise, inv_noise])
    weighted = (particles.astype(jnp.float32) * ctf_both * noise_both[None, :]).astype(jnp.bfloat16)
    ctf_power = (ctf * ctf * inv_noise[None, :]).astype(jnp.bfloat16)
    packed = jnp.concatenate([weighted, ctf_power], axis=1)
    real_part = references[:, :coef].astype(jnp.float32)
    imag_part = references[:, coef:].astype(jnp.float32)
    power = (real_part * real_part + imag_part * imag_part).astype(jnp.bfloat16)
    dims = (((1,), (1,)), ((), ()))
    piece = lax.all_gather(packed, "orient", axis=0, tiled=True)
    cross = lax.dot_general(piece[:, :feat], references, dims, preferred_element_type=jnp.float32)
    energy = lax.dot_general(piece[:, feat:], power, dims, preferred_element_type=jnp.float32)
    scores = cross - 0.5 * energy
    local_top = jnp.max(scores, axis=1)
    local_sum = jnp.sum(jnp.exp(scores - local_top[:, None]), axis=1)
    all_tops, all_sums = (
        lax.all_gather(local_top[None, :], "orient", axis=0, tiled=True),
        lax.all_gather(local_sum[None, :], "orient", axis=0, tiled=True),
    )
    top_score = jnp.max(all_tops, axis=0)
    scaled = all_sums * jnp.exp(all_tops - top_score[None, :])
    total = jnp.sum(scaled, axis=0)
    ranks = jnp.arange(all_tops.shape[0], dtype=jnp.int32)
    earlier_rows = (ranks < lax.axis_index("orient"))[:, None]
    shifted = jnp.sum(jnp.where(earlier_rows, scaled, 0.0), axis=0)
    expon = jnp.exp(scores - top_score[:, None])
    posterior = expon / total[:, None]
    row_ids = lax.broadcasted_iota(jnp.int32, (ori_dev, ori_dev), 0)
    col_ids = lax.broadcasted_iota(jnp.int32, (ori_dev, ori_dev), 1)
    upper = (row_ids <= col_ids).astype(jnp.float32)
    running = jnp.dot(
        expon, upper, precision=lax.Precision.HIGHEST, preferred_element_type=jnp.float32
    )
    cumulative = (shifted[:, None] + running) / total[:, None]
    before = cumulative - posterior
    fraction = thresholds.astype(jnp.float32) / 1024.0
    kept = jnp.minimum(jnp.maximum(fraction[:, None] - before, 0.0), posterior)
    all_orients = lax.axis_size("orient") * ori_dev
    orient_ids = lax.axis_index("orient") * ori_dev + jnp.arange(ori_dev, dtype=jnp.int32)
    inside = (orient_ids[None, :] - range_start[:, None]) % all_orients < range_len[:, None]
    local_kept = jnp.sum(jnp.where(inside, kept, 0.0), axis=1)
    kept_mass = lax.psum(local_kept, "orient")
    log_evidence = top_score + jnp.log(total)
    return (posterior, cumulative, log_evidence, kept_mass)


def solution(mesh):
    return jax.shard_map(
        on_device,
        mesh=mesh,
        in_specs=(
            P(("dom", "orient"), None),
            P(("dom", "orient")),
            P(),
            P(("dom", "orient"), None),
            P("dom"),
            P("dom"),
            P("dom"),
        ),
        out_specs=(P("dom", "orient"), P("dom", "orient"), P("dom"), P("dom")),
        check_vma=False,
    )
```

profile of v0, /device:TPU:0, one launch (start us, length us, event | category | flops | bytes accessed | tf_op | source)
XLA Modules:
  0.0 113.0 jit_solution(12283271416409016182)
XLA Ops:
  7.2 0.0 all-gather.4.cloned.1.call-start
  7.2 0.8 pad_maximum_fusion.1
  8.0 1.3 %fusion.7 = (f32[8,4224]{1,0:T(8,128)S(1)}, bf16[8,4224]{1,0:T(8,128)(2,1)S(1)}) fusion(f32[4224]{0:T(1024)S(1)} %fusion.23, f32[8]{0:T(128)} %param.8, f32[4224]{0:T(1024)} %param.9), kind=kLoop, calls=%fused_computation.16 | loop fusion | flops 202752 | bytes 236576 | tf_op jit(solution)/shard_map/neg | solution.py:14
  9.3 1.0 fusion.6
  10.3 0.7 pad_maximum_fusion
  11.0 0.0 all-gather.4.cloned.1.call-update
  11.0 1.2 %dynamic-slice = u32[1]{0:T(128)} dynamic-slice(u32[32]{0:T(128)} %constant.75, u32[]{:T(128)S(6)} %add.76), dynamic_slice_sizes={1} | dynamic-slice | bytes 12
  12.9 0.7 convert_multiply_fusion
  13.6 45.1 %all-gather.4.cloned.1.call-done = bf16[64,12672]{1,0:T(8,128)(2,1)} async-done(((bf16[8,12672]{1,0:T(8,128)(2,1)}), bf16[64,12672]{1,0:T(8,128)(2,1)}) %all-gather.4.cloned.1.call-update) | async-done | bytes 1622032 | tf_op jit(solution)/shard_map/all_gather | solution.py:31
  58.7 5.0 %fusion.2 = f32[64,432]{1,0:T(8,128)S(1)} fusion(bf16[432,8448]{1,0:T(8,128)(2,1)} %param.10, bf16[64,12672]{1,0:T(8,128)(2,1)} %all-gather.4.cloned.1.call-done), kind=kOutput, calls=%fused_computation.5 | convolution fusion | flops 244546560 | bytes 7950336 | tf_op jit(solution)/shard_map/dot_general | solution.py:33
  63.6 0.4 copy-done
  64.0 0.4 copy-done.1
  64.5 2.3 %fusion.30 = (f32[64]{0:T(128)S(1)}, f32[64,432]{1,0:T(8,128)S(1)}) fusion(f32[64,432]{1,0:T(8,128)S(1)} %fusion.2, bf16[432,8448]{1,0:T(8,128)(2,1)S(1)} %copy-done, bf16[64,12672]{1,0:T(8,128)(2,1)S(1)} %copy-done.1), kind=kOutput, calls=%fused_computation.53 | convolution fusion | flops 467195840 | bytes 8622336 | tf_op jit(solution)/shard_map/dot_general | solution.py:32
  66.8 0.2 exponential_reduce_fusion
  67.0 0.2 dynamic-update-slice
  67.2 0.2 dynamic-update-slice.1
  67.4 18.8 %all-reduce.2 = (f32[512]{0:T(512)S(1)}, f32[512]{0:T(512)S(1)}) all-reduce(f32[512]{0:T(512)S(1)} %dynamic-update-slice.1, f32[512]{0:T(512)S(1)} %dynamic-update-slice), channel_id=3, replica_groups=mesh['orient'=8,'dom'=4] {'orient'}, use_global_device_ids=true, to_apply=%add.1 | all-reduce | flops 1024 | bytes 8192
  86.2 0.1 reshape.54
  86.3 0.1 reshape.55
  86.4 0.1 select_reduce_fusion.1
  86.4 0.5 log_add_fusion
  87.0 0.0 copy-done.2
  87.0 1.2 %select_reduce_fusion = (f32[64]{0:T(128)S(1)}, f32[64,432]{1,0:T(8,128)}, f32[64,432]{1,0:T(8,128)}) fusion(f32[64]{0:T(128)S(1)} %convert_multiply_fusion, s32[64]{0:T(128)S(1)} %copy-done.2, s32[64]{0:T(128)S(1)} %copy-done.3, s32[432]{0:T(512)S(1)} %iota_add_fusion, f32[64]{0:T(128)S(1)} %get-tuple-element.5, f32[64,432]{1,0:T(8,128)S(1)} %get-tuple-element.13, ...), kind=kOutput, calls=%fused_computation.18 | convolution fusion | flops 144039104 | bytes 335296 | tf_op jit(solution)/shard_map/dot_general | solution.py:52
  88.1 18.0 %psum.7 = f32[64]{0:T(128)} all-reduce(f32[64]{0:T(128)S(1)} %get-tuple-element.8), channel_id=1, replica_groups=mesh['orient'=8,'dom'=4] {'orient'}, use_global_device_ids=true, to_apply=%region_6.7 | all-reduce | flops 64 | bytes 512 | tf_op jit(solution)/shard_map/psum | solution.py:63
  (11 shorter events, 0.1 us)
Async XLA Ops:
  7.2 51.5 %all-gather.4.cloned.1.call-start = ((), (), s32[]{:S(2)}) async-start(), calls=%async_computation | async-start | bytes 1824768 | tf_op jit(solution)/shard_map/all_gather | solution.py:31
  58.6 5.4 %copy-start = (bf16[432,8448]{1,0:T(8,128)(2,1)S(1)}, bf16[432,8448]{1,0:T(8,128)(2,1)}, u32[]{:S(2)}) copy-start(bf16[432,8448]{1,0:T(8,128)(2,1)} %param.10) | copy-start | bytes 21897220
  58.7 5.8 %copy-start.1 = (bf16[64,12672]{1,0:T(8,128)(2,1)S(1)}, bf16[64,12672]{1,0:T(8,128)(2,1)}, u32[]{:S(2)}) copy-start(bf16[64,12672]{1,0:T(8,128)(2,1)} %all-gather.4.cloned.1.call-done) | copy-start | bytes 4866052
  64.4 22.5 %copy-start.2 = (s32[64]{0:T(128)S(1)}, s32[64]{0:T(128)}, u32[]{:S(2)}) copy-start(s32[64]{0:T(128)} %param.13) | copy-start | bytes 772
  64.4 22.5 %copy-start.3 = (s32[64]{0:T(128)S(1)}, s32[64]{0:T(128)}, u32[]{:S(2)}) copy-start(s32[64]{0:T(128)} %param.12) | copy-start | bytes 772
Sparse Core Ops, SparseCore 0:
  11.1 47.4 all-gather.3
where the time goes:
time: 113 us
  waiting for transfers between devices  45.1 us (40%)
  blocking collectives  36.7 us (32%)
  between operations  14.7 us (13%)
  matrix products  8.47 us (7%)
  other arithmetic  5.25 us (5%)
  local copies, waits for them, and re-layouts  2.66 us (2%)
    all_gather x1, waiting for transfers between devices, on_device(): piece = lax.all_gather(packed, 'orient', axis=0, tiled=True)  45.1 us
    unnamed x1, blocking collectives  18.8 us
    psum x1, blocking collectives, on_device(): kept_mass = lax.psum(local_kept, 'orient')  18 us
    dot_general x1, matrix products, on_device(): lax.dot_general(piece[:, feat:], power, dims, preferred_element_type=jnp....  4.98 us
    unnamed x13, local copies, waits for them, and re-layouts  2.51 us
    dot_general x1, matrix products, on_device(): lax.dot_general(piece[:, :feat], references, dims, preferred_element_type...  2.33 us
  transfers between devices with their start and end apart: 1, of which 1 were waited for; matrix products, arithmetic and copies ran while one was open for 2% of the time, Pallas kernels for 0%

commit v1 on v0

v1 whole, which is shorter than its diff:
```python
import functools
import math

import jax
import jax.numpy as jnp
from jax import lax
from jax.experimental import pallas as pl
from jax.experimental.pallas import tpu as pltpu
from jax.sharding import PartitionSpec as P

MESH = pl.DeviceIdType.MESH
DIMS = (((1,), (1,)), ((), ()))
PIECES = 3
ROWS = 16


def sin_of(x):
    k = jnp.floor(x * (1.0 / math.pi) + 0.5)
    r = x - k * 3.140625
    r = r - k * 9.67502593994140625e-4
    r = r - k * 1.509957990978376432e-7
    s = r * r
    p = jnp.float32(-2.3889859e-8)
    p = p * s + 2.7525562e-6
    p = p * s - 1.9840874e-4
    p = p * s + 8.3333310e-3
    p = p * s - 1.6666667e-1
    y = r + r * s * p
    half = k * 0.5
    return jnp.where(half == jnp.floor(half), y, -y)


def loop(count, body):
    if count <= 4:
        for i in range(count):
            body(i)
    else:
        def step(i, carry):
            body(i)
            return carry
        lax.fori_loop(0, count, step, 0)


def kernel(
    n, particles, defocus, noise, references, thresholds, starts, lens,
    posterior, cumulative, evidence, kept_mass,
    gath, dgath, refs, ctf, ctf_power, power, weighted, acc, expon, prefix, mine, sgath,
    own_sem, ref_sem, z_send, z_recv, y_send, y_recv, d_send, d_recv, s_send, s_recv,
):
    wide = 2 if n % 2 == 0 else 1
    deep = n // wide
    per = particles.shape[0]
    feat = particles.shape[1]
    coef = feat // 2
    size = coef // PIECES
    chunks = 2 * PIECES
    ori = references.shape[0]
    total_ori = n * ori
    parts = n * per
    me = lax.axis_index("orient")
    row = lax.div(me, wide)
    col = lax.rem(me, wide)

    def cut(c):
        return pl.ds(c * size, size)

    def peer(t):
        return lax.rem(me + t, n)

    barrier = pltpu.get_barrier_semaphore()
    for t in range(1, n):
        pl.semaphore_signal(barrier, inc=1, device_id={"orient": peer(t)}, device_id_type=MESH)

    own = pltpu.make_async_copy(particles, gath.at[me], own_sem.at[0])
    own.start()
    own_d = pltpu.make_async_copy(defocus, dgath.at[me], own_sem.at[1])
    own_d.start()
    order = [c for k in range(PIECES) for c in (k, k + PIECES)]
    loads = {}
    for c in order:
        loads[c] = pltpu.make_async_copy(references.at[:, cut(c)], refs.at[:, cut(c)], ref_sem.at[c])
        loads[c].start()
    own.wait()
    own_d.wait()
    pl.semaphore_wait(barrier, n - 1)

    def d_copy(source, target):
        return pltpu.make_async_remote_copy(
            src_ref=dgath.at[source], dst_ref=dgath.at[source],
            send_sem=d_send.at[target], recv_sem=d_recv.at[source],
            device_id={"orient": target}, device_id_type=MESH)

    def z_copy(c, source_row, target_row):
        block = gath.at[source_row * wide + col, :, cut(c)]
        return pltpu.make_async_remote_copy(
            src_ref=block, dst_ref=block,
            send_sem=z_send.at[c, target_row], recv_sem=z_recv.at[c, source_row],
            device_id={"orient": target_row * wide + col}, device_id_type=MESH)

    def y_copy(c, source_row, source_col):
        block = gath.at[source_row * wide + source_col, :, cut(c)]
        return pltpu.make_async_remote_copy(
            src_ref=block, dst_ref=block,
            send_sem=y_send.at[c, source_row], recv_sem=y_recv.at[c, source_row],
            device_id={"orient": row * wide + (wide - 1 - col)}, device_id_type=MESH)

    def s_copy(source, target):
        return pltpu.make_async_remote_copy(
            src_ref=mine, dst_ref=sgath.at[source],
            send_sem=s_send.at[target], recv_sem=s_recv.at[source],
            device_id={"orient": target}, device_id_type=MESH)

    for t in range(1, n):
        d_copy(me, peer(t)).start()
    other_rows = [lax.rem(row + t, deep) for t in range(1, deep)]
    for c in order:
        if wide == 2:
            y_copy(c, row, col).start()
        for r in other_rows:
            z_copy(c, row, r).start()

    def relay(c):
        for r in other_rows:
            z_copy(c, r, r).wait_recv()
            if wide == 2:
                y_copy(c, r, col).start()

    def arrived(c):
        if wide == 2:
            y_copy(c, row, col).wait_recv()
            for r in other_rows:
                y_copy(c, r, col).wait_recv()

    eye8 = lax.broadcasted_iota(jnp.int32, (per, per), 0) == lax.broadcasted_iota(jnp.int32, (per, per), 1)
    group = max(1, ROWS // per)

    def ctf_piece(k):
        index = k * size + lax.broadcasted_iota(jnp.int32, (1, size), 1)
        row_pos = lax.shift_right_logical(index, 7).astype(jnp.float32)
        col_pos = ((index & 127) - 64).astype(jnp.float32)
        freq = math.pi * (row_pos * row_pos + col_pos * col_pos) / 16384.0
        noise_row = noise[:, cut(k)]

        def body(i):
            columns = []
            for j in range(group):
                line = dgath[i * group + j]
                columns.append(jnp.sum(jnp.where(eye8, line, 0.0), axis=1, keepdims=True))
            d = jnp.concatenate(columns, axis=0)
            value = -sin_of(d * freq + 0.07)
            rows = pl.ds(pl.multiple_of(i * ROWS, ROWS), ROWS)
            ctf[rows, cut(k)] = value
            ctf_power[rows, cut(k)] = (value * value * noise_row).astype(jnp.bfloat16)

        loop(parts // ROWS, body)

    def energy_piece(k):
        loads[k].wait()
        loads[k + PIECES].wait()

        def body(i):
            rows = pl.ds(pl.multiple_of(i * ROWS, ROWS), ROWS)
            re = refs[rows, cut(k)].astype(jnp.float32)
            im = refs[rows, cut(k + PIECES)].astype(jnp.float32)
            power[rows, :] = (re * re + im * im).astype(jnp.bfloat16)

        loop(ori // ROWS, body)
        term = -0.5 * lax.dot_general(ctf_power[:, cut(k)], power[...], DIMS, preferred_element_type=jnp.float32)
        if k == 0:
            acc[...] = term
        else:
            acc[...] += term

    def cross_piece(c):
        k = c % PIECES
        noise_row = noise[:, cut(k)]

        def body(i):
            rows = pl.ds(pl.multiple_of(i * ROWS, ROWS), ROWS)
            block = gath[pl.ds(i * group, group), :, cut(c)].astype(jnp.float32).reshape(ROWS, size)
            weighted[rows, :] = (block * ctf[rows, cut(k)] * noise_row).astype(jnp.bfloat16)

        loop(parts // ROWS, body)
        acc[...] += lax.dot_general(weighted[...], refs[:, cut(c)], DIMS, preferred_element_type=jnp.float32)

    for t in range(1, n):
        d_copy(peer(t), me).wait_recv()
    for k in range(PIECES):
        ctf_piece(k)
        relay(order[2 * k])
        energy_piece(k)
        relay(order[2 * k + 1])
    for c in order:
        arrived(c)
        cross_piece(c)

    scores = acc[...]
    top = jnp.max(scores, axis=1, keepdims=True)
    e = jnp.exp(scores - top)
    expon[:, :ori] = e
    eye = lax.broadcasted_iota(jnp.int32, (parts, parts), 0) == lax.broadcasted_iota(jnp.int32, (parts, parts), 1)

    def to_col(x):
        return jnp.sum(jnp.where(eye, x, 0), axis=1, keepdims=True)

    def to_row(x):
        return jnp.sum(jnp.where(eye, x, 0.0), axis=0, keepdims=True)

    start = to_col(starts[...])
    length = to_col(lens[...])
    ids = me * ori + lax.broadcasted_iota(jnp.int32, (parts, ori), 1)
    rel = ids - start
    inside = jnp.where(rel < 0, rel + total_ori, rel) < length
    first = me * ori - start
    first_inside = jnp.where(first < 0, first + total_ori, first) < length
    in_range = jnp.sum(jnp.where(inside, e, 0.0), axis=1, keepdims=True)
    ahead = jnp.sum(jnp.where(rel < 0, e, 0.0), axis=1, keepdims=True)
    ahead = jnp.where(first_inside, 0.0, ahead)
    for i, value in enumerate((top, jnp.sum(e, axis=1, keepdims=True), in_range, ahead)):
        line = to_row(value)
        mine[i : i + 1, :] = line
        sgath[me, i : i + 1, :] = line
    for t in range(1, n):
        s_copy(me, peer(t)).start()

    lanes = 128
    blocks = expon.shape[1] // lanes
    if ori < expon.shape[1]:
        expon[:, ori:] = jnp.zeros((parts, expon.shape[1] - ori), jnp.float32)
    upper = (
        lax.broadcasted_iota(jnp.int32, (lanes, lanes), 0) <= lax.broadcasted_iota(jnp.int32, (lanes, lanes), 1)
    ).astype(jnp.bfloat16)
    carry = jnp.zeros((parts, 1), jnp.float32)
    for b in range(blocks):
        x = expon[:, b * lanes : (b + 1) * lanes]
        high = x.astype(jnp.bfloat16)
        rest = x - high.astype(jnp.float32)
        mid = rest.astype(jnp.bfloat16)
        low = (rest - mid.astype(jnp.float32)).astype(jnp.bfloat16)
        run = carry
        for piece in (low, mid, high):
            run = run + jnp.dot(piece, upper, preferred_element_type=jnp.float32)
        prefix[:, b * lanes : (b + 1) * lanes] = run
        carry = run[:, lanes - 1 : lanes]

    for c in order:
        for r in other_rows:
            z_copy(c, row, r).wait_send()
            if wide == 2:
                y_copy(c, r, col).wait_send()
        if wide == 2:
            y_copy(c, row, col).wait_send()
    for t in range(1, n):
        d_copy(me, peer(t)).wait_send()
        s_copy(me, peer(t)).wait_send()
    for t in range(1, n):
        s_copy(peer(t), me).wait_recv()

    stats = [sgath[s] for s in range(n)]
    best = stats[0][0:1]
    for s in stats[1:]:
        best = jnp.maximum(best, s[0:1])
    scale = [jnp.exp(s[0:1] - best) for s in stats]
    base = jnp.zeros_like(best)
    my_base = base
    bases = []
    for s in range(n):
        my_base = jnp.where(me == s, base, my_base)
        bases.append(base)
        base = base + scale[s] * stats[s][1:2]
    total = base
    limit = thresholds[...].astype(jnp.float32) / 1024.0 * total
    kept = jnp.zeros_like(best)
    for s in range(n):
        left = limit - bases[s] - scale[s] * stats[s][3:4]
        kept = kept + jnp.minimum(jnp.maximum(left, 0.0), scale[s] * stats[s][2:3])
    kept_mass[...] = kept / total
    evidence[...] = best + jnp.log(total)
    my_scale = to_col(jnp.exp(mine[0:1, :] - best) / total)
    my_base = to_col(my_base / total)
    posterior[...] = expon[:, :ori] * my_scale
    cumulative[...] = my_base + prefix[:, :ori] * my_scale


def on_device(n, particles, defocus, inv_noise, references, thresholds, range_start, range_len):
    per, feat = particles.shape
    coef = feat // 2
    ori = references.shape[0]
    parts = n * per
    padded = -(-ori // 128) * 128
    chunks = 2 * PIECES
    deep = n // 2 if n % 2 == 0 else n
    f32, bf16 = jnp.float32, jnp.bfloat16
    vmem = pl.BlockSpec(memory_space=pltpu.VMEM)
    hbm = pl.BlockSpec(memory_space=pl.ANY)
    dma = pltpu.SemaphoreType.DMA
    outs = pl.pallas_call(
        functools.partial(kernel, n),
        out_shape=(
            jax.ShapeDtypeStruct((parts, ori), f32),
            jax.ShapeDtypeStruct((parts, ori), f32),
            jax.ShapeDtypeStruct((1, parts), f32),
            jax.ShapeDtypeStruct((1, parts), f32),
        ),
        in_specs=[hbm, hbm, vmem, hbm, vmem, vmem, vmem],
        out_specs=[vmem] * 4,
        scratch_shapes=[
            pltpu.VMEM((n, per, feat), bf16),
            pltpu.VMEM((n, 1, per), f32),
            pltpu.VMEM((ori, feat), bf16),
            pltpu.VMEM((parts, coef), f32),
            pltpu.VMEM((parts, coef), bf16),
            pltpu.VMEM((ori, coef // PIECES), bf16),
            pltpu.VMEM((parts, coef // PIECES), bf16),
            pltpu.VMEM((parts, ori), f32),
            pltpu.VMEM((parts, padded), f32),
            pltpu.VMEM((parts, padded), f32),
            pltpu.VMEM((4, parts), f32),
            pltpu.VMEM((n, 4, parts), f32),
            dma((2,)),
            dma((chunks,)),
            dma((chunks, deep)),
            dma((chunks, deep)),
            dma((chunks, deep)),
            dma((chunks, deep)),
            dma((n,)),
            dma((n,)),
            dma((n,)),
            dma((n,)),
        ],
        compiler_params=pltpu.CompilerParams(
            collective_id=0, has_side_effects=True, vmem_limit_bytes=56 * 1024 * 1024
        ),
    )(
        particles, defocus.reshape(1, per), inv_noise.reshape(1, coef), references,
        thresholds.reshape(1, parts), range_start.reshape(1, parts), range_len.reshape(1, parts),
    )
    return outs[0], outs[1], outs[2].reshape(parts), outs[3].reshape(parts)


def solution(mesh):
    return jax.shard_map(
        functools.partial(on_device, mesh.shape["orient"]),
        mesh=mesh,
        in_specs=(
            P(("dom", "orient"), None),
            P(("dom", "orient")),
            P(),
            P(("dom", "orient"), None),
            P("dom"),
            P("dom"),
            P("dom"),
        ),
        out_specs=(P("dom", "orient"), P("dom", "orient"), P("dom"), P("dom")),
        check_vma=False,
    )
```

time: 113 us -> 38.6 us (0.34)
  waiting for transfers between devices: 45.1 us -> 0 us
  blocking collectives: 36.7 us -> 0 us
  Pallas kernels: 0 us -> 31 us
  between operations: 14.7 us -> 0.64 us
  matrix products: 8.47 us -> 0 us
  other arithmetic: 5.25 us -> 0 us
  local copies, waits for them, and re-layouts: 2.66 us -> 6.69 us
    all_gather x1 -> x0, waiting for transfers between devices: 45.1 us -> none  [on_device(): piece = lax.all_gather(packed, 'orient', axis=0, tiled=True)]
    pallas_call x0 -> x1, Pallas kernels: none -> 31 us  [on_device(): pl.pallas_call(functools.partial(kernel, n), out_shape=(jax.ShapeDtypeStr...]
    unnamed x1 -> x0, blocking collectives: 18.8 us -> none
    psum x1 -> x0, blocking collectives: 18 us -> none  [on_device(): kept_mass = lax.psum(local_kept, 'orient')]
    dot_general x3 -> x0, matrix products: 8.47 us -> none  [the longest x1 4.98 us: on_device(): lax.dot_general(piece[:, feat:], power, dims, preferred_element_type=jnp....]
    unnamed x13 -> x4, local copies, waits for them, and re-layouts: 2.51 us -> 5.35 us
    concatenate x2 -> x0, other arithmetic: 1.52 us -> none  [the longest x1 0.81 us: on_device(): noise_both = jnp.concatenate([inv_noise, inv_noise])]
    reshape x0 -> x1, local copies, waits for them, and re-layouts: none -> 1.35 us  [on_device(): inv_noise.reshape(1, coef)]
  transfers between devices with their start and end apart: 1 -> 0, of which waited for: 1 -> 0; matrix products, arithmetic and copies ran while one was open for 2% -> 0% of each run, Pallas kernels for 0% -> 0%
where the time goes in v1:
time: 38.6 us; the launch traced here: 38.3 us
  Pallas kernels  31 us (80%)
  local copies, waits for them, and re-layouts  6.69 us (17%)
  between operations  0.64 us (2%)
    pallas_call x1, Pallas kernels, on_device(): pl.pallas_call(functools.partial(kernel, n), out_shape=(jax.ShapeDtypeStr...  31 us
    unnamed x4, local copies, waits for them, and re-layouts  5.35 us
    reshape x1, local copies, waits for them, and re-layouts, on_device(): inv_noise.reshape(1, coef)  1.35 us

profile of v1, /device:TPU:0, one launch (start us, length us, event | category | flops | bytes accessed | tf_op | source)
XLA Modules:
  0.0 38.3 jit_solution(4645566440366757275)
XLA Ops:
  0.6 1.3 %reshape.30.noise = f32[1,4224]{1,0:T(1,128)} reshape(f32[4224]{0:T(1024)} %param.9) | data formatting | bytes 33792 | tf_op jit(solution)/shard_map/reshape | solution.py:335
  2.0 31.0 %shard_map.102 = (f32[64,432]{1,0:T(8,128)}, f32[64,432]{1,0:T(8,128)}, f32[1,64]{1,0:T(1,128)}, f32[1,64]{1,0:T(1,128)}) custom-call(bf16[8,8448]{1,0:T(8,128)(2,1)} %particles.1, f32[1,8]{1,0:T(1,128)} %bitcast.6, f32[1,4224]{1,0:T(1,128)} %reshape.30.noise, bf16[432,8448]{1,0:T(8,128)(2,1)} %references.1, s32[1,64]{1,0:T(1,128)} %bitcast.7, ...), custom_call_target="tpu_custom_call" | custom-call | tf_op jit(solution)/shard_map/pallas_call | solution.py:297
  32.9 1.6 %copy.15 = f32[64,432]{1,0:T(8,128)} copy(f32[64,432]{1,0:T(8,128)} %get-tuple-element.16) | data formatting | bytes 221184
  34.5 1.6 %copy.16 = f32[64,432]{1,0:T(8,128)} copy(f32[64,432]{1,0:T(8,128)} %get-tuple-element.17) | data formatting | bytes 221184
  36.1 1.1 %copy.17 = f32[64]{0:T(128)} copy(f32[64]{0:T(128)} %bitcast.11) | data formatting | bytes 512
  37.2 1.1 %copy.18 = f32[64]{0:T(128)} copy(f32[64]{0:T(128)} %bitcast.10) | data formatting | bytes 512

commit v2 on v1

v2 whole, which is shorter than its diff:
```python
import functools
import math

import jax
import jax.numpy as jnp
from jax import lax
from jax.experimental import pallas as pl
from jax.experimental.pallas import tpu as pltpu
from jax.sharding import PartitionSpec as P

MESH = pl.DeviceIdType.MESH
DIMS = (((1,), (1,)), ((), ()))
PIECES = 3
ROWS = 16


def sin_of(x):
    k = jnp.floor(x * (1.0 / math.pi) + 0.5)
    r = x - k * 3.140625
    r = r - k * 9.67502593994140625e-4
    r = r - k * 1.509957990978376432e-7
    s = r * r
    p = jnp.float32(-2.3889859e-8)
    p = p * s + 2.7525562e-6
    p = p * s - 1.9840874e-4
    p = p * s + 8.3333310e-3
    p = p * s - 1.6666667e-1
    y = r + r * s * p
    half = k * 0.5
    return jnp.where(half == jnp.floor(half), y, -y)


def loop(count, body):
    if count <= 4:
        for i in range(count):
            body(i)
    else:
        def step(i, carry):
            body(i)
            return carry
        lax.fori_loop(0, count, step, 0)


def kernel(
    n, particles, defocus, noise_hbm, references, starts_hbm, lens_hbm,
    expon_hbm, prefix_hbm, sgath,
    gath, dgath, refs, ctf, ctf_power, power, weighted, acc, mine, expon, prefix, noise, starts, lens,
    own_sem, ref_sem, up_send, down_send, side_send, recv, dup_send, ddown_send, dside_send, d_recv, s_send, s_recv,
):
    wide = 2
    deep = n // wide
    per = particles.shape[0]
    feat = particles.shape[1]
    coef = feat // 2
    size = coef // PIECES
    ori = references.shape[0]
    total_ori = n * ori
    parts = n * per
    group = wide * per
    me = lax.axis_index("orient")
    row = lax.div(me, wide)
    col = lax.rem(me, wide)
    partner = row * wide + (1 - col)
    has_up = row + 1 < deep
    has_down = row > 0

    def cut(c):
        return pl.ds(c * size, size)

    def peer(t):
        return lax.rem(me + t, n)

    def near(act):
        act(partner)

        @pl.when(has_up)
        def _():
            act(me + wide)

        @pl.when(has_down)
        def _():
            act(me - wide)

    barrier = pltpu.get_barrier_semaphore()

    def greet(target):
        pl.semaphore_signal(barrier, inc=1, device_id={"orient": target}, device_id_type=MESH)

    near(greet)
    order = [c for k in range(PIECES) for c in (k, k + PIECES)]
    paired = order[-1]
    own = pltpu.make_async_copy(particles, gath.at[me], own_sem.at[0])
    own.start()
    own_d = pltpu.make_async_copy(defocus, dgath.at[me], own_sem.at[1])
    own_d.start()
    loads = {}
    for c in order:
        loads[c] = pltpu.make_async_copy(references.at[:, cut(c)], refs.at[:, cut(c)], ref_sem.at[c])
        loads[c].start()
    small = [
        pltpu.make_async_copy(noise_hbm, noise, own_sem.at[2]),
        pltpu.make_async_copy(starts_hbm, starts, own_sem.at[3]),
        pltpu.make_async_copy(lens_hbm, lens, own_sem.at[4]),
    ]
    for copy in small:
        copy.start()
    own.wait()
    own_d.wait()
    pl.semaphore_wait(barrier, 1 + has_up.astype(jnp.int32) + has_down.astype(jnp.int32))

    def remote(block, send_sem, recv_sem, target):
        return pltpu.make_async_remote_copy(
            src_ref=block, dst_ref=block, send_sem=send_sem, recv_sem=recv_sem,
            device_id={"orient": target}, device_id_type=MESH)

    def up(c, source):
        if c is None:
            return remote(dgath.at[source], dup_send.at[source], d_recv.at[source], me + wide)
        return remote(gath.at[source, :, cut(c)], up_send.at[c, source], recv.at[c, source], me + wide)

    def down(c, source):
        if c is None:
            return remote(dgath.at[source], ddown_send.at[source], d_recv.at[source], me - wide)
        return remote(gath.at[source, :, cut(c)], down_send.at[c, source], recv.at[c, source], me - wide)

    def side(c, source):
        if c is None:
            return remote(dgath.at[source], dside_send.at[source], d_recv.at[source], partner)
        return remote(gath.at[source, :, cut(c)], side_send.at[c, source], recv.at[c, source], partner)

    def s_copy(source, target):
        return pltpu.make_async_remote_copy(
            src_ref=mine, dst_ref=sgath.at[source],
            send_sem=s_send.at[target], recv_sem=s_recv.at[source],
            device_id={"orient": target}, device_id_type=MESH)

    def both(c, source):
        @pl.when(has_up)
        def _():
            up(c, source).start()

        @pl.when(has_down)
        def _():
            down(c, source).start()

    side(None, me).start()
    both(None, me)
    for c in [paired] + order[:-1]:
        side(c, me).start()
    for c in order:
        both(c, me)

    def handle(c, t):
        @pl.when(row >= t)
        def _():
            for column in (col, 1 - col) if c == paired else (col,):
                source = (row - t) * wide + column
                side(c, source).wait_recv()

                @pl.when(has_up)
                def _():
                    up(c, source).start()

                if c != paired:
                    side(c, source).start()

        @pl.when(row + t < deep)
        def _():
            for column in (col, 1 - col) if c == paired else (col,):
                source = (row + t) * wide + column
                side(c, source).wait_recv()

                @pl.when(has_down)
                def _():
                    down(c, source).start()

                if c != paired:
                    side(c, source).start()

    def arrived(c):
        if c != paired:
            for r in range(deep):
                side(c, r * wide + 1 - col).wait_recv()

    eye8 = lax.broadcasted_iota(jnp.int32, (per, per), 0) == lax.broadcasted_iota(jnp.int32, (per, per), 1)

    def ctf_row(r, wait=True):
        if wait:
            side(None, r * wide + 1 - col).wait_recv()
        columns = []
        for j in range(wide):
            columns.append(jnp.sum(jnp.where(eye8, dgath[r * wide + j], 0.0), axis=1, keepdims=True))
        d = jnp.concatenate(columns, axis=0)
        rows = pl.ds(pl.multiple_of(r * group, group), group)

        def body(k):
            index = k * size + lax.broadcasted_iota(jnp.int32, (1, size), 1)
            row_pos = lax.shift_right_logical(index, 7).astype(jnp.float32)
            col_pos = ((index & 127) - 64).astype(jnp.float32)
            freq = math.pi * (row_pos * row_pos + col_pos * col_pos) / 16384.0
            value = -sin_of(d * freq + 0.07)
            ctf[rows, cut(k)] = value
            ctf_power[rows, cut(k)] = (value * value * noise[cut(k)].reshape(1, size)).astype(jnp.bfloat16)

        for k in range(PIECES):
            body(k)

    def ctf_rows(t):
        @pl.when(row >= t)
        def _():
            ctf_row(row - t)

        @pl.when(row + t < deep)
        def _():
            ctf_row(row + t)

    def power_piece(k):
        loads[k].wait()
        loads[k + PIECES].wait()

        def body(i):
            rows = pl.ds(pl.multiple_of(i * ROWS, ROWS), ROWS)
            re = refs[rows, cut(k)].astype(jnp.float32)
            im = refs[rows, cut(k + PIECES)].astype(jnp.float32)
            power[rows, cut(k)] = (re * re + im * im).astype(jnp.bfloat16)

        loop(ori // ROWS, body)

    def energy_piece(k):
        term = -0.5 * lax.dot_general(
            ctf_power[:, cut(k)], power[:, cut(k)], DIMS, preferred_element_type=jnp.float32)
        if k == 0:
            acc[...] = term
        else:
            acc[...] += term

    def cross_piece(c):
        k = c % PIECES

        def body(i):
            rows = pl.ds(pl.multiple_of(i * group, group), group)
            block = gath[pl.ds(i * wide, wide), :, cut(c)].astype(jnp.float32).reshape(group, size)
            weighted[rows, :] = (block * ctf[rows, cut(k)] * noise[cut(k)].reshape(1, size)).astype(jnp.bfloat16)

        loop(deep, body)
        acc[...] += lax.dot_general(weighted[...], refs[:, cut(c)], DIMS, preferred_element_type=jnp.float32)

    short = deep == 4
    power_piece(0)
    power_piece(1)
    for copy in small:
        copy.wait()
    side(paired, partner).wait_recv()
    both(paired, partner)
    if short:
        tasks = {
            (1, 0): [lambda: ctf_row(row)], (1, 3): [lambda: power_piece(2)],
            (1, 5): [lambda: ctf_rows(1)], (2, 3): [lambda: ctf_rows(2)],
        }
        last = [lambda: ctf_rows(3)]
        last += [functools.partial(energy_piece, k) for k in range(PIECES)]
        for i, task in enumerate(last):
            tasks.setdefault((deep - 1, min(1 + i, len(order) - 1)), []).append(task)
    else:
        tasks = {(1, 0): [lambda: power_piece(2)]}
    for t in range(1, deep):
        handle(None, t)
        for i, c in enumerate(order):
            handle(c, t)
            for task in tasks.get((t, i), ()):
                task()
    if not short:
        for r in range(deep):
            side(None, r * wide + 1 - col).wait_recv()
        loop(deep, lambda r: ctf_row(r, wait=False))
        for k in range(PIECES):
            energy_piece(k)
    for c in order:
        arrived(c)
        cross_piece(c)

    scores = acc[...]
    top = jnp.max(scores, axis=1, keepdims=True)
    e = jnp.exp(scores - top)
    expon[:, :ori] = e
    eye = lax.broadcasted_iota(jnp.int32, (parts, parts), 0) == lax.broadcasted_iota(jnp.int32, (parts, parts), 1)

    def to_col(x):
        return jnp.sum(jnp.where(eye, x, 0), axis=1, keepdims=True)

    def to_row(x):
        return jnp.sum(jnp.where(eye, x, 0.0), axis=0, keepdims=True)

    start = to_col(starts[...])
    length = to_col(lens[...])
    ids = me * ori + lax.broadcasted_iota(jnp.int32, (parts, ori), 1)
    rel = ids - start
    inside = jnp.where(rel < 0, rel + total_ori, rel) < length
    first = me * ori - start
    first_inside = jnp.where(first < 0, first + total_ori, first) < length
    in_range = jnp.sum(jnp.where(inside, e, 0.0), axis=1, keepdims=True)
    ahead = jnp.sum(jnp.where(rel < 0, e, 0.0), axis=1, keepdims=True)
    ahead = jnp.where(first_inside, 0.0, ahead)
    for i, value in enumerate((top, jnp.sum(e, axis=1, keepdims=True), in_range, ahead)):
        line = to_row(value)
        mine[i : i + 1, :] = line
        sgath[me, i : i + 1, :] = line
    for t in range(1, n):
        s_copy(me, peer(t)).start()

    lanes = 128
    blocks = expon.shape[1] // lanes
    if ori < expon.shape[1]:
        expon[:, ori:] = jnp.zeros((parts, expon.shape[1] - ori), jnp.float32)
    upper = (
        lax.broadcasted_iota(jnp.int32, (lanes, lanes), 0) <= lax.broadcasted_iota(jnp.int32, (lanes, lanes), 1)
    ).astype(jnp.bfloat16)
    carry = jnp.zeros((parts, 1), jnp.float32)
    for b in range(blocks):
        x = expon[:, b * lanes : (b + 1) * lanes]
        high = x.astype(jnp.bfloat16)
        rest = x - high.astype(jnp.float32)
        mid = rest.astype(jnp.bfloat16)
        low = (rest - mid.astype(jnp.float32)).astype(jnp.bfloat16)
        run = carry
        for piece in (low, mid, high):
            run = run + jnp.dot(piece, upper, preferred_element_type=jnp.float32)
        prefix[:, b * lanes : (b + 1) * lanes] = run
        carry = run[:, lanes - 1 : lanes]

    outs = [
        pltpu.make_async_copy(expon, expon_hbm, own_sem.at[0]),
        pltpu.make_async_copy(prefix, prefix_hbm, own_sem.at[1]),
    ]
    for copy in outs:
        copy.start()

    def drain(c, source, along, across):
        if along:
            @pl.when(has_up & (lax.div(source, wide) <= row))
            def _():
                up(c, source).wait_send()

            @pl.when(has_down & (lax.div(source, wide) >= row))
            def _():
                down(c, source).wait_send()

        if across:
            side(c, source).wait_send()

    for c in [None] + order:
        for r in range(deep):
            drain(c, r * wide + col, True, c != paired)
            if c == paired:
                drain(c, r * wide + 1 - col, True, False)
    side(paired, me).wait_send()
    for t in range(1, n):
        s_copy(me, peer(t)).wait_send()
    for copy in outs:
        copy.wait()
    for t in range(1, n):
        s_copy(peer(t), me).wait_recv()


def finish(n, expon, prefix, sgath, thresholds, posterior, cumulative, evidence, kept_mass):
    parts, ori = posterior.shape
    me = lax.axis_index("orient")
    eye = lax.broadcasted_iota(jnp.int32, (parts, parts), 0) == lax.broadcasted_iota(jnp.int32, (parts, parts), 1)

    def to_col(x):
        return jnp.sum(jnp.where(eye, x, 0), axis=1, keepdims=True)

    stats = [sgath[s] for s in range(n)]
    best = stats[0][0:1]
    for s in stats[1:]:
        best = jnp.maximum(best, s[0:1])
    scale = [jnp.exp(s[0:1] - best) for s in stats]
    base = jnp.zeros_like(best)
    my_base = base
    bases = []
    for s in range(n):
        my_base = jnp.where(me == s, base, my_base)
        bases.append(base)
        base = base + scale[s] * stats[s][1:2]
    total = base
    limit = thresholds[...].astype(jnp.float32) / 1024.0 * total
    kept = jnp.zeros_like(best)
    for s in range(n):
        left = limit - bases[s] - scale[s] * stats[s][3:4]
        kept = kept + jnp.minimum(jnp.maximum(left, 0.0), scale[s] * stats[s][2:3])
    kept_mass[...] = kept / total
    evidence[...] = best + jnp.log(total)
    my_scale = to_col(jnp.exp(sgath[me, 0:1, :] - best) / total)
    my_base = to_col(my_base / total)
    posterior[...] = expon[:, :ori] * my_scale
    cumulative[...] = my_base + prefix[:, :ori] * my_scale


def on_device(n, particles, defocus, inv_noise, references, thresholds, range_start, range_len):
    per, feat = particles.shape
    coef = feat // 2
    ori = references.shape[0]
    parts = n * per
    padded = -(-ori // 128) * 128
    chunks = 2 * PIECES
    f32, bf16 = jnp.float32, jnp.bfloat16
    vmem = pl.BlockSpec(memory_space=pltpu.VMEM)
    hbm = pl.BlockSpec(memory_space=pl.ANY)
    dma = pltpu.SemaphoreType.DMA
    expon, prefix, stats = pl.pallas_call(
        functools.partial(kernel, n),
        out_shape=(
            jax.ShapeDtypeStruct((parts, padded), f32),
            jax.ShapeDtypeStruct((parts, padded), f32),
            jax.ShapeDtypeStruct((n, 4, parts), f32),
        ),
        in_specs=[hbm] * 6,
        out_specs=[hbm, hbm, vmem],
        scratch_shapes=[
            pltpu.VMEM((n, per, feat), bf16),
            pltpu.VMEM((n, 1, per), f32),
            pltpu.VMEM((ori, feat), bf16),
            pltpu.VMEM((parts, coef), f32),
            pltpu.VMEM((parts, coef), bf16),
            pltpu.VMEM((ori, coef), bf16),
            pltpu.VMEM((parts, coef // PIECES), bf16),
            pltpu.VMEM((parts, ori), f32),
            pltpu.VMEM((4, parts), f32),
            pltpu.VMEM((parts, padded), f32),
            pltpu.VMEM((parts, padded), f32),
            pltpu.VMEM((coef,), f32),
            pltpu.VMEM((1, parts), jnp.int32),
            pltpu.VMEM((1, parts), jnp.int32),
            dma((5,)),
            dma((chunks,)),
            dma((chunks, n)),
            dma((chunks, n)),
            dma((chunks, n)),
            dma((chunks, n)),
            dma((n,)),
            dma((n,)),
            dma((n,)),
            dma((n,)),
            dma((n,)),
            dma((n,)),
        ],
        compiler_params=pltpu.CompilerParams(
            collective_id=0, has_side_effects=True, vmem_limit_bytes=56 * 1024 * 1024
        ),
    )(
        particles, defocus.reshape(1, per), inv_noise, references,
        range_start.reshape(1, parts), range_len.reshape(1, parts),
    )
    outs = pl.pallas_call(
        functools.partial(finish, n),
        out_shape=(
            jax.ShapeDtypeStruct((parts, ori), f32),
            jax.ShapeDtypeStruct((parts, ori), f32),
            jax.ShapeDtypeStruct((1, parts), f32),
            jax.ShapeDtypeStruct((1, parts), f32),
        ),
        in_specs=[vmem] * 4,
        out_specs=[vmem] * 4,
    )(expon, prefix, stats, thresholds.reshape(1, parts))
    return outs[0], outs[1], outs[2].reshape(parts), outs[3].reshape(parts)


def solution(mesh):
    return jax.shard_map(
        functools.partial(on_device, mesh.shape["orient"]),
        mesh=mesh,
        in_specs=(
            P(("dom", "orient"), None),
            P(("dom", "orient")),
            P(),
            P(("dom", "orient"), None),
            P("dom"),
            P("dom"),
            P("dom"),
        ),
        out_specs=(P("dom", "orient"), P("dom", "orient"), P("dom"), P("dom")),
        check_vma=False,
    )
```

time: 38.6 us -> 32.1 us (0.83)
  local copies, waits for them, and re-layouts: 6.69 us -> 0 us
    unnamed x4 -> x0, local copies, waits for them, and re-layouts: 5.35 us -> none
    pallas_call x0 -> x1, Pallas kernels: none -> 1.79 us  [on_device(): pl.pallas_call(functools.partial(finish, n), out_shape=(jax.ShapeDtypeStr...]
    pallas_call x1, Pallas kernels: 31 us -> 29.5 us  [on_device(): pl.pallas_call(functools.partial(kernel, n), out_shape=(jax.ShapeDtypeStr...]
    reshape x1 -> x0, local copies, waits for them, and re-layouts: 1.35 us -> none  [on_device(): inv_noise.reshape(1, coef)]
where the time goes in v2:
time: 32.1 us; the launch traced here: 32 us
  Pallas kernels  31.3 us (98%)
  between operations  0.64 us (2%)
    pallas_call x1, Pallas kernels, on_device(): pl.pallas_call(functools.partial(kernel, n), out_shape=(jax.ShapeDtypeStr...  29.5 us
    pallas_call x1, Pallas kernels, on_device(): pl.pallas_call(functools.partial(finish, n), out_shape=(jax.ShapeDtypeStr...  1.79 us

profile of v2, /device:TPU:0, one launch (start us, length us, event | category | flops | bytes accessed | tf_op | source)
XLA Modules:
  0.0 32.0 jit_solution(16191333194595398715)
XLA Ops:
  0.6 29.5 %shard_map.102 = (f32[64,512]{1,0:T(8,128)}, f32[64,512]{1,0:T(8,128)}, f32[8,4,64]{2,1,0:T(4,128)}) custom-call(bf16[8,8448]{1,0:T(8,128)(2,1)} %particles.1, f32[1,8]{1,0:T(1,128)} %bitcast.6, f32[4224]{0:T(1024)} %noise_hbm.1, bf16[432,8448]{1,0:T(8,128)(2,1)} %references.1, s32[1,64]{1,0:T(1,128)} %bitcast.7, s32[1,64]{1,0:T(1,128)} %bitcast.8), custom_call_target="tpu_custom_call" | custom-call | tf_op jit(solution)/shard_map/pallas_call | solution.py:410
  30.2 1.8 %shard_map.103 = (f32[64,432]{1,0:T(8,128)}, f32[64,432]{1,0:T(8,128)}, f32[1,64]{1,0:T(1,128)}, f32[1,64]{1,0:T(1,128)}) custom-call(f32[64,512]{1,0:T(8,128)} %get-tuple-element.11.expon, f32[64,512]{1,0:T(8,128)} %get-tuple-element.12.prefix, f32[8,4,64]{2,1,0:T(4,128)} %get-tuple-element.13.sgath, s32[1,64]{1,0:T(1,128)} %bitcast.9), custom_call_target="tpu_custom_call" | custom-call | tf_op jit(solution)/shard_map/pallas_call | solution.py:454

commit v3 on v2

--- a/solution.py
+++ b/solution.py
@@ -11,6 +11,7 @@
 MESH = pl.DeviceIdType.MESH
 DIMS = (((1,), (1,)), ((), ()))
 PIECES = 3
+SPANS = ((0, 4), (4, 6))
 ROWS = 16
 
 
@@ -67,6 +68,9 @@
     def cut(c):
         return pl.ds(c * size, size)
 
+    def span(c):
+        return pl.ds(SPANS[c][0] * size, (SPANS[c][1] - SPANS[c][0]) * size)
+
     def peer(t):
         return lax.rem(me + t, n)
 
@@ -87,14 +91,15 @@
         pl.semaphore_signal(barrier, inc=1, device_id={"orient": target}, device_id_type=MESH)
 
     near(greet)
-    order = [c for k in range(PIECES) for c in (k, k + PIECES)]
-    paired = order[-1]
+    order = list(range(len(SPANS)))
+    paired = -1
+    pieces = [c for k in range(PIECES) for c in (k, k + PIECES)]
     own = pltpu.make_async_copy(particles, gath.at[me], own_sem.at[0])
     own.start()
     own_d = pltpu.make_async_copy(defocus, dgath.at[me], own_sem.at[1])
     own_d.start()
     loads = {}
-    for c in order:
+    for c in pieces:
         loads[c] = pltpu.make_async_copy(references.at[:, cut(c)], refs.at[:, cut(c)], ref_sem.at[c])
         loads[c].start()
     small = [
@@ -116,17 +121,17 @@
     def up(c, source):
         if c is None:
             return remote(dgath.at[source], dup_send.at[source], d_recv.at[source], me + wide)
-        return remote(gath.at[source, :, cut(c)], up_send.at[c, source], recv.at[c, source], me + wide)
+        return remote(gath.at[source, :, span(c)], up_send.at[c, source], recv.at[c, source], me + wide)
 
     def down(c, source):
         if c is None:
             return remote(dgath.at[source], ddown_send.at[source], d_recv.at[source], me - wide)
-        return remote(gath.at[source, :, cut(c)], down_send.at[c, source], recv.at[c, source], me - wide)
+        return remote(gath.at[source, :, span(c)], down_send.at[c, source], recv.at[c, source], me - wide)
 
     def side(c, source):
         if c is None:
             return remote(dgath.at[source], dside_send.at[source], d_recv.at[source], partner)
-        return remote(gath.at[source, :, cut(c)], side_send.at[c, source], recv.at[c, source], partner)
+        return remote(gath.at[source, :, span(c)], side_send.at[c, source], recv.at[c, source], partner)
 
     def s_copy(source, target):
         return pltpu.make_async_remote_copy(
@@ -145,7 +150,7 @@
 
     side(None, me).start()
     both(None, me)
-    for c in [paired] + order[:-1]:
+    for c in order:
         side(c, me).start()
     for c in order:
         both(c, me)
@@ -250,17 +255,14 @@
     power_piece(1)
     for copy in small:
         copy.wait()
-    side(paired, partner).wait_recv()
-    both(paired, partner)
     if short:
         tasks = {
-            (1, 0): [lambda: ctf_row(row)], (1, 3): [lambda: power_piece(2)],
-            (1, 5): [lambda: ctf_rows(1)], (2, 3): [lambda: ctf_rows(2)],
+            (1, 0): [lambda: ctf_row(row)],
+            (1, 1): [lambda: power_piece(2), lambda: ctf_rows(1)],
+            (2, 1): [lambda: ctf_rows(2)],
+            (3, 0): [lambda: ctf_rows(3), lambda: energy_piece(0)],
+            (3, 1): [lambda: energy_piece(1), lambda: energy_piece(2)],
         }
-        last = [lambda: ctf_rows(3)]
-        last += [functools.partial(energy_piece, k) for k in range(PIECES)]
-        for i, task in enumerate(last):
-            tasks.setdefault((deep - 1, min(1 + i, len(order) - 1)), []).append(task)
     else:
         tasks = {(1, 0): [lambda: power_piece(2)]}
     for t in range(1, deep):
@@ -277,7 +279,8 @@
             energy_piece(k)
     for c in order:
         arrived(c)
-        cross_piece(c)
+        for piece in range(*SPANS[c]):
+            cross_piece(piece)
 
     scores = acc[...]
     top = jnp.max(scores, axis=1, keepdims=True)
@@ -353,7 +356,6 @@
             drain(c, r * wide + col, True, c != paired)
             if c == paired:
                 drain(c, r * wide + 1 - col, True, False)
-    side(paired, me).wait_send()
     for t in range(1, n):
         s_copy(me, peer(t)).wait_send()
     for copy in outs:
@@ -433,10 +435,10 @@
             pltpu.VMEM((1, parts), jnp.int32),
             dma((5,)),
             dma((chunks,)),
-            dma((chunks, n)),
-            dma((chunks, n)),
-            dma((chunks, n)),
-            dma((chunks, n)),
+            dma((len(SPANS), n)),
+            dma((len(SPANS), n)),
+            dma((len(SPANS), n)),
+            dma((len(SPANS), n)),
             dma((n,)),
             dma((n,)),
             dma((n,)),

time: 32.1 us -> 30.2 us (0.941)
  Pallas kernels: 31.3 us -> 29.4 us
    pallas_call x1, Pallas kernels: 29.5 us -> 27.6 us  [on_device(): pl.pallas_call(functools.partial(kernel, n), out_shape=(jax.ShapeDtypeStr...]
where the time goes in v3:
time: 30.2 us; the launch traced here: 30 us
  Pallas kernels  29.4 us (97%)
  between operations  0.64 us (2%)
    pallas_call x1, Pallas kernels, on_device(): pl.pallas_call(functools.partial(kernel, n), out_shape=(jax.ShapeDtypeStr...  27.6 us
    pallas_call x1, Pallas kernels, on_device(): pl.pallas_call(functools.partial(finish, n), out_shape=(jax.ShapeDtypeStr...  1.79 us

profile of v3, /device:TPU:0, one launch (start us, length us, event | category | flops | bytes accessed | tf_op | source)
XLA Modules:
  0.0 30.0 jit_solution(4804940652004812125)
XLA Ops:
  0.6 27.6 %shard_map.102 = (f32[64,512]{1,0:T(8,128)}, f32[64,512]{1,0:T(8,128)}, f32[8,4,64]{2,1,0:T(4,128)}) custom-call(bf16[8,8448]{1,0:T(8,128)(2,1)} %particles.1, f32[1,8]{1,0:T(1,128)} %bitcast.6, f32[4224]{0:T(1024)} %noise_hbm.1, bf16[432,8448]{1,0:T(8,128)(2,1)} %references.1, s32[1,64]{1,0:T(1,128)} %bitcast.7, s32[1,64]{1,0:T(1,128)} %bitcast.8), custom_call_target="tpu_custom_call" | custom-call | tf_op jit(solution)/shard_map/pallas_call | solution.py:412
  28.2 1.8 %shard_map.103 = (f32[64,432]{1,0:T(8,128)}, f32[64,432]{1,0:T(8,128)}, f32[1,64]{1,0:T(1,128)}, f32[1,64]{1,0:T(1,128)}) custom-call(f32[64,512]{1,0:T(8,128)} %get-tuple-element.11.expon, f32[64,512]{1,0:T(8,128)} %get-tuple-element.12.prefix, f32[8,4,64]{2,1,0:T(4,128)} %get-tuple-element.13.sgath, s32[1,64]{1,0:T(1,128)} %bitcast.9), custom_call_target="tpu_custom_call" | custom-call | tf_op jit(solution)/shard_map/pallas_call | solution.py:456
